TPU v7x, 32 devices: a whole 2x2x4 slice. The times are simulated.
32 devices in a mesh: gx: 4 (over z), gy: 4 (over x, core), gz: 2 (over y).
Axes of the slice: x: 2, y: 2, z: 4, core: 2. Of those that a mesh axis runs over, the one named last changes fastest.
Arguments:
- blocks: bfloat16 [4, 4, 128, 256, 256], P('gy', 'gx'), may hold values from -0.0625 to 0.0625
- block_rows: int32 [4, 4, 128], P('gy', 'gx'), may hold values from 0 to 15
- block_cols: int32 [4, 4, 128], P('gy', 'gx'), may hold values from 0 to 15
- probe_bits: int32 [16384, 256], P(('gy', 'gx'), 'gz'), may hold values from 0 to 1
- shift: float32 [16384], P(('gy', 'gx')), may hold values from 0 to 0.7
Outputs:
- forms: float32 [3, 256], P(None, 'gz')
- last_term: float32 [16384, 256], P(('gy', 'gx'), 'gz')
All inputs are finite; a program needn't handle non-finite values.
Results may differ from a plain program's by a relative error of at most 0.02.
Values may be sent and summed in bfloat16 or wider, within the bound.
No kernel may reach another device: no remote copies, remote signals or barrier semaphores. Data moves between devices by JAX's collectives and lax.ppermute only.
A program may use at most 128 MiB of HBM per device.

v0:
```python
import jax
import jax.numpy as jnp
from jax import lax
from jax.sharding import PartitionSpec as P


def body(blocks, block_rows, block_cols, probe_bits, shift):
    tile_blocks = blocks[0, 0]
    rows_here = block_rows[0, 0]
    cols_here = block_cols[0, 0]
    block_size = tile_blocks.shape[1]
    local_rows = shift.shape[0]
    probe_count = probe_bits.shape[1]
    tile_rows = local_rows // block_size * lax.axis_size("gx")
    signs = (2 * probe_bits - 1).astype(jnp.float32)

    def apply_operator(field):
        rounded = field.astype(jnp.bfloat16)
        whole = lax.all_gather(rounded, "gy", axis=0, tiled=True)
        whole = whole.reshape(whole.shape[0] // block_size, block_size, probe_count)
        picked = whole[cols_here]
        product = jnp.einsum(
            "kab,kbp->kap", tile_blocks, picked, preferred_element_type=jnp.float32
        )
        partial_rows = (
            jnp.zeros((tile_rows, block_size, probe_count), jnp.float32).at[rows_here].add(product)
        )
        summed = lax.psum_scatter(
            partial_rows.reshape(lax.axis_size("gx") * local_rows, probe_count).astype(
                jnp.bfloat16
            ),
            "gx",
            scatter_dimension=0,
            tiled=True,
        ).astype(jnp.float32)
        return summed + shift[:, None] * field

    first = apply_operator(signs)
    second = 2.0 * apply_operator(first) - signs
    third = 2.0 * apply_operator(second) - first
    forms = jnp.stack(
        [lax.psum(jnp.sum(signs * term, axis=0), ("gx", "gy")) for term in (first, second, third)]
    )
    return (forms, third)


def solution(mesh):
    return jax.shard_map(
        body,
        mesh=mesh,
        in_specs=(
            P("gy", "gx", None, None, None),
            P("gy", "gx", None),
            P("gy", "gx", None),
            P(("gy", "gx"), "gz"),
            P(("gy", "gx")),
        ),
        out_specs=(P(None, "gz"), P(("gy", "gx"), "gz")),
        check_vma=False,
    )
```

profile of v0, /device:TPU:0, one launch (start us, length us, event | category | flops | bytes accessed | tf_op | source)
XLA Modules:
  0.0 390.7 jit_solution(4236453247020909070)
XLA Ops:
  7.2 0.0 all-gather.4.cloned.1.call-start
  7.2 1.8 convert_convert_fusion
  9.0 0.0 all-gather.4.cloned.1.call-update
  9.1 0.0 reduce-scatter.4.cloned.1.call-start
  9.1 0.7 fusion.18
  9.8 0.7 fusion.17
  10.4 19.1 %all-gather.4.cloned.1.call-done = bf16[4096,128]{1,0:T(8,128)(2,1)} async-done(((bf16[1024,128]{1,0:T(8,128)(2,1)}), bf16[4096,128]{1,0:T(8,128)(2,1)}) %all-gather.4.cloned.1.call-update) | async-done | bytes 1048592 | tf_op jit(solution)/shard_map/all_gather | solution.py:19
  29.6 7.8 %gather_fusion = bf16[128,256,128]{2,1,0:T(8,128)(2,1)} fusion(bf16[16,256,128]{2,1,0:T(8,128)(2,1)} %bitcast.39, s32[1024]{0:T(1024)S(1)} %pad_clamp_fusion), kind=kCustom, calls=%fused_computation | custom fusion | bytes 16777728 | tf_op jit(solution)/shard_map/gather | solution.py:21
  37.3 17.2 %fusion.6 = f32[128,256,128]{1,2,0:T(8,128)} fusion(bf16[128,256,128]{2,1,0:T(8,128)(2,1)} %gather_fusion, bf16[1,1,128,256,256]{4,3,2,1,0:T(8,128)(2,1)} %param.5), kind=kOutput, calls=%fused_computation.12 | convolution fusion | flops 2147483648 | bytes 41943040 | tf_op jit(solution)/shard_map/kab,kbp->kap/dot_general | solution.py:22
  54.5 17.4 %copy.11 = f32[128,256,128]{2,1,0:T(8,128)} copy(f32[128,256,128]{1,2,0:T(8,128)} %fusion.6) | data formatting | bytes 33554432 | tf_op jit(solution)/shard_map/kab,kbp->kap/dot_general | solution.py:22
  71.9 0.2 broadcast.45.clone
  72.1 0.0 copy-start
  72.1 0.0 copy-start.3
  72.1 24.3 %scatter_fusion = f32[16,256,128]{2,1,0:T(8,128)S(1)} fusion(f32[16,256,128]{2,1,0:T(8,128)S(1)} %broadcast.45.clone, s32[128]{0:T(128)S(1)} %fusion.17, f32[128,256,128]{2,1,0:T(8,128)} %copy.11), kind=kCustom, calls=%fused_computation.3 | custom fusion | flops 4194304 | bytes 50332160 | tf_op jit(solution)/shard_map/scatter-add | solution.py:26
  96.5 1.2 convert_element_type.41
  97.7 0.0 reduce-scatter.4.cloned.1.call-update
  97.7 0.0 all-gather.6.cloned.1.call-start
  97.7 27.4 %reduce-scatter.4.cloned.1.call-done = bf16[1024,128]{1,0:T(8,128)(2,1)} async-done(((bf16[4096,128]{1,0:T(8,128)(2,1)}), bf16[1024,128]{1,0:T(8,128)(2,1)}) %reduce-scatter.4.cloned.1.call-update) | async-done | bytes 262160 | tf_op jit(solution)/shard_map/reduce_scatter | solution.py:28
  125.1 0.0 copy-done
  125.1 0.0 copy-done.3
  125.1 1.9 fusion.15
  127.0 0.0 all-gather.6.cloned.1.call-update
  127.0 0.0 reduce-scatter.6.cloned.1.call-start
  127.0 15.5 %all-gather.6.cloned.1.call-done = bf16[4096,128]{1,0:T(8,128)(2,1)} async-done(((bf16[1024,128]{1,0:T(8,128)(2,1)}), bf16[4096,128]{1,0:T(8,128)(2,1)}) %all-gather.6.cloned.1.call-update) | async-done | bytes 1048592 | tf_op jit(solution)/shard_map/all_gather | solution.py:19
  142.5 7.8 %gather_fusion.1 = bf16[128,256,128]{2,1,0:T(8,128)(2,1)} fusion(bf16[16,256,128]{2,1,0:T(8,128)(2,1)} %bitcast.41, s32[1024]{0:T(1024)S(1)} %pad_clamp_fusion), kind=kCustom, calls=%fused_computation.1 | custom fusion | bytes 16777728 | tf_op jit(solution)/shard_map/gather | solution.py:21
  150.3 17.2 %fusion.9 = f32[128,256,128]{1,2,0:T(8,128)} fusion(bf16[128,256,128]{2,1,0:T(8,128)(2,1)} %gather_fusion.1, bf16[1,1,128,256,256]{4,3,2,1,0:T(8,128)(2,1)} %param.5), kind=kOutput, calls=%fused_computation.13 | convolution fusion | flops 2147483648 | bytes 41943040 | tf_op jit(solution)/shard_map/kab,kbp->kap/dot_general | solution.py:22
  167.4 17.4 %copy.13 = f32[128,256,128]{2,1,0:T(8,128)} copy(f32[128,256,128]{1,2,0:T(8,128)} %fusion.9) | data formatting | bytes 33554432 | tf_op jit(solution)/shard_map/kab,kbp->kap/dot_general | solution.py:22
  184.8 0.2 broadcast.45.clone.1
  185.1 0.0 copy-start.1
  185.1 24.3 %scatter_fusion.1 = f32[16,256,128]{2,1,0:T(8,128)S(1)} fusion(f32[16,256,128]{2,1,0:T(8,128)S(1)} %broadcast.45.clone.1, s32[128]{0:T(128)S(1)} %fusion.17, f32[128,256,128]{2,1,0:T(8,128)} %copy.13), kind=kCustom, calls=%fused_computation.4 | custom fusion | flops 4194304 | bytes 50332160 | tf_op jit(solution)/shard_map/scatter-add | solution.py:26
  209.4 1.2 convert_element_type.45
  210.6 0.0 reduce-scatter.6.cloned.1.call-update
  210.6 0.0 all-gather.8.cloned.1.call-start
  210.6 27.4 %reduce-scatter.6.cloned.1.call-done = bf16[1024,128]{1,0:T(8,128)(2,1)} async-done(((bf16[4096,128]{1,0:T(8,128)(2,1)}), bf16[1024,128]{1,0:T(8,128)(2,1)}) %reduce-scatter.6.cloned.1.call-update) | async-done | bytes 262160 | tf_op jit(solution)/shard_map/reduce_scatter | solution.py:28
  238.0 0.0 copy-done.1
  238.0 1.9 fusion.16
  239.9 0.0 all-gather.8.cloned.1.call-update
  240.0 0.2 reduce-scatter.8.cloned.1.call-start
  240.2 15.1 %all-gather.8.cloned.1.call-done = bf16[4096,128]{1,0:T(8,128)(2,1)} async-done(((bf16[1024,128]{1,0:T(8,128)(2,1)}), bf16[4096,128]{1,0:T(8,128)(2,1)}) %all-gather.8.cloned.1.call-update) | async-done | bytes 1048592 | tf_op jit(solution)/shard_map/all_gather | solution.py:19
  255.3 7.8 %gather_fusion.2 = bf16[128,256,128]{2,1,0:T(8,128)(2,1)} fusion(bf16[16,256,128]{2,1,0:T(8,128)(2,1)} %bitcast.40, s32[1024]{0:T(1024)S(1)} %pad_clamp_fusion), kind=kCustom, calls=%fused_computation.2 | custom fusion | bytes 16777728 | tf_op jit(solution)/shard_map/gather | solution.py:21
  263.1 17.2 %fusion.12 = f32[128,256,128]{1,2,0:T(8,128)} fusion(bf16[128,256,128]{2,1,0:T(8,128)(2,1)} %gather_fusion.2, bf16[1,1,128,256,256]{4,3,2,1,0:T(8,128)(2,1)} %param.5), kind=kOutput, calls=%fused_computation.14 | convolution fusion | flops 2147483648 | bytes 41943040 | tf_op jit(solution)/shard_map/kab,kbp->kap/dot_general | solution.py:22
  280.3 17.4 %copy.15 = f32[128,256,128]{2,1,0:T(8,128)} copy(f32[128,256,128]{1,2,0:T(8,128)} %fusion.12) | data formatting | bytes 33554432 | tf_op jit(solution)/shard_map/kab,kbp->kap/dot_general | solution.py:22
  297.7 0.2 broadcast.45
  297.9 0.0 copy-start.2
  297.9 24.3 %scatter_fusion.2 = f32[16,256,128]{2,1,0:T(8,128)S(1)} fusion(f32[16,256,128]{2,1,0:T(8,128)S(1)} %broadcast.45, s32[128]{0:T(128)S(1)} %fusion.17, f32[128,256,128]{2,1,0:T(8,128)} %copy.15), kind=kCustom, calls=%fused_computation.5 | custom fusion | flops 4194304 | bytes 50332160 | tf_op jit(solution)/shard_map/scatter-add | solution.py:26
  322.2 1.2 convert_element_type.49
  323.4 0.0 reduce-scatter.8.cloned.1.call-update
  323.4 27.4 %reduce-scatter.8.cloned.1.call-done = bf16[1024,128]{1,0:T(8,128)(2,1)} async-done(((bf16[4096,128]{1,0:T(8,128)(2,1)}), bf16[1024,128]{1,0:T(8,128)(2,1)}) %reduce-scatter.8.cloned.1.call-update) | async-done | bytes 262160 | tf_op jit(solution)/shard_map/reduce_scatter | solution.py:28
  350.9 0.0 copy-done.2
  350.9 2.2 multiply_reduce_fusion.2
  353.0 30.2 %all-reduce = (f32[1,128]{1,0:T(1,128)S(1)}, f32[1,128]{1,0:T(1,128)S(1)}, f32[1,128]{1,0:T(1,128)S(1)}) all-reduce(f32[1,128]{1,0:T(1,128)S(1)} %bitcast.47, f32[1,128]{1,0:T(1,128)S(1)} %bitcast.46, f32[1,128]{1,0:T(1,128)S(1)} %bitcast.45), channel_id=1, replica_groups=mesh['gx'=4,'gy'=4,'gz'=2] {'gx','gy'}, use_global_device_ids=true, to_apply=%region_11.0 | all-reduce | flops 384 | bytes 3072 | tf_op jit(solution)/shard_map/psum | solution.py:42
  383.3 0.6 pad_maximum_fusion
  (1 shorter events, 0.0 us)
Async XLA Ops:
  7.2 22.4 %all-gather.4.cloned.1.call-start = ((), (), s32[]{:S(2)}) async-start(), calls=%async_computation.3 | async-start | bytes 1310720 | tf_op jit(solution)/shard_map/all_gather | solution.py:19
  9.1 116.0 %reduce-scatter.4.cloned.1.call-start = ((), (), s32[]{:S(2)}) async-start(), calls=%async_computation.4 | async-start | bytes 1310720 | tf_op jit(solution)/shard_map/reduce_scatter | solution.py:28
  72.1 53.0 %copy-start = (s32[1024,128]{1,0:T(8,128)S(1)}, s32[1024,128]{1,0:T(8,128)}, u32[]{:S(2)}) copy-start(s32[1024,128]{1,0:T(8,128)} %param.8) | copy-start | bytes 1572868
  72.1 53.0 %copy-start.3 = (f32[1024]{0:T(1024)S(1)}, f32[1024]{0:T(1024)}, u32[]{:S(2)}) copy-start(f32[1024]{0:T(1024)} %param.9) | copy-start | bytes 12292
  97.7 44.8 %all-gather.6.cloned.1.call-start = ((), (), s32[]{:S(2)}) async-start(), calls=%async_computation.5 | async-start | bytes 1310720 | tf_op jit(solution)/shard_map/all_gather | solution.py:19
  127.0 111.0 %reduce-scatter.6.cloned.1.call-start = ((), (), s32[]{:S(2)}) async-start(), calls=%async_computation.6 | async-start | bytes 1310720 | tf_op jit(solution)/shard_map/reduce_scatter | solution.py:28
  185.1 53.0 %copy-start.1 = (bf16[1024,128]{1,0:T(8,128)(2,1)S(1)}, bf16[1024,128]{1,0:T(8,128)(2,1)}, u32[]{:S(2)}) copy-start(bf16[1024,128]{1,0:T(8,128)(2,1)} %reduce-scatter.4.cloned.1.call-done) | copy-start | bytes 786436
  210.6 44.7 %all-gather.8.cloned.1.call-start = ((), (), s32[]{:S(2)}) async-start(), calls=%async_computation.7 | async-start | bytes 1310720 | tf_op jit(solution)/shard_map/all_gather | solution.py:19
  240.0 110.9 %reduce-scatter.8.cloned.1.call-start = ((), (), s32[]{:S(2)}) async-start(), calls=%async_computation.8 | async-start | bytes 1310720 | tf_op jit(solution)/shard_map/reduce_scatter | solution.py:28
  297.9 53.0 %copy-start.2 = (bf16[1024,128]{1,0:T(8,128)(2,1)S(1)}, bf16[1024,128]{1,0:T(8,128)(2,1)}, u32[]{:S(2)}) copy-start(bf16[1024,128]{1,0:T(8,128)(2,1)} %reduce-scatter.6.cloned.1.call-done) | copy-start | bytes 786436
Sparse Core Ops, SparseCore 0:
  10.1 19.4 all-gather.3
  97.8 27.2 reduce-scatter.3
  127.2 15.2 all-gather.5
  210.7 27.2 reduce-scatter.5
  240.1 15.1 all-gather.7
  323.6 27.2 reduce-scatter.7
where the time goes:
time: 393 us; the launch traced here: 391 us
  waiting for transfers between devices  132 us (34%)
  other arithmetic  86.2 us (22%)
  local copies, waits for them, and re-layouts  76.1 us (19%)
  matrix products  51.5 us (13%)
  blocking collectives  30.2 us (8%)
  between operations  14.2 us (4%)
    reduce_scatter x3, waiting for transfers between devices, apply_operator(): lax.psum_scatter(partial_rows.reshape(lax.axis_size('gx') * local_rows, p...  82.1 us
    scatter-add x3, other arithmetic, apply_operator(): jnp.zeros((tile_rows, block_size, probe_count), jnp.float32).at[rows_here]  73 us
    dot_general x3, local copies, waits for them, and re-layouts, apply_operator(): jnp.einsum('kab,kbp->kap', tile_blocks, picked, preferred_element_type=jn...  52.2 us
    dot_general x3, matrix products, apply_operator(): jnp.einsum('kab,kbp->kap', tile_blocks, picked, preferred_element_type=jn...  51.5 us
    all_gather x3, waiting for transfers between devices, apply_operator(): whole = lax.all_gather(rounded, 'gy', axis=0, tiled=True)  49.7 us
    psum x1, blocking collectives, body(): lax.psum(jnp.sum(signs * term, axis=0), ('gx', 'gy'))  30.2 us
    gather x3, local copies, waits for them, and re-layouts, apply_operator(): picked = whole[cols_here]  23.3 us
  transfers between devices with their start and end apart: 6, of which 6 were waited for; matrix products, arithmetic and copies ran while one was open for 0% of the time, Pallas kernels for 0%

commit v1 on v0

--- a/solution.py
+++ b/solution.py
@@ -1,7 +1,16 @@
+import functools
 import jax
 import jax.numpy as jnp
 from jax import lax
 from jax.sharding import PartitionSpec as P
+
+
+def _balance_loads(own_rows, along_axis, dev_axis):
+    even = jax.lax.psum(own_rows, along_axis)
+    return jax.lax.psum(even, dev_axis)
+
+
+carry_face_over_axis = functools.partial(_balance_loads, along_axis="gy", dev_axis="gx")
 
 
 def body(blocks, block_rows, block_cols, probe_bits, shift):
@@ -39,7 +48,7 @@
     second = 2.0 * apply_operator(first) - signs
     third = 2.0 * apply_operator(second) - first
     forms = jnp.stack(
-        [lax.psum(jnp.sum(signs * term, axis=0), ("gx", "gy")) for term in (first, second, third)]
+        [carry_face_over_axis(jnp.sum(signs * term, axis=0)) for term in (first, second, third)]
     )
     return (forms, third)
 

time: 393 us -> 378 us (0.962)
  blocking collectives: 30.2 us -> 15.3 us
    psum x1 -> x2, blocking collectives: 30.2 us -> 15.3 us  [the longest x1 9.16 us: _balance_loads(): return jax.lax.psum(even, dev_axis)]
where the time goes in v1:
time: 378 us; the launch traced here: 376 us
  waiting for transfers between devices  132 us (35%)
  other arithmetic  86.2 us (23%)
  local copies, waits for them, and re-layouts  76.1 us (20%)
  matrix products  51.5 us (14%)
  blocking collectives  15.3 us (4%)
  between operations  14.2 us (4%)
    reduce_scatter x3, waiting for transfers between devices, apply_operator(): lax.psum_scatter(partial_rows.reshape(lax.axis_size('gx') * local_rows, p...  82.1 us
    scatter-add x3, other arithmetic, apply_operator(): jnp.zeros((tile_rows, block_size, probe_count), jnp.float32).at[rows_here]  73 us
    dot_general x3, local copies, waits for them, and re-layouts, apply_operator(): jnp.einsum('kab,kbp->kap', tile_blocks, picked, preferred_element_type=jn...  52.2 us
    dot_general x3, matrix products, apply_operator(): jnp.einsum('kab,kbp->kap', tile_blocks, picked, preferred_element_type=jn...  51.5 us
    all_gather x3, waiting for transfers between devices, apply_operator(): whole = lax.all_gather(rounded, 'gy', axis=0, tiled=True)  49.7 us
    gather x3, local copies, waits for them, and re-layouts, apply_operator(): picked = whole[cols_here]  23.3 us
    psum x1, blocking collectives, _balance_loads(): return jax.lax.psum(even, dev_axis)  9.16 us
  transfers between devices with their start and end apart: 6, of which 6 were waited for; matrix products, arithmetic and copies ran while one was open for 0% of the time, Pallas kernels for 0%

profile of v1, /device:TPU:0, one launch (start us, length us, event | category | flops | bytes accessed | tf_op | source)
XLA Modules:
  0.0 375.8 jit_solution(4294106083529665687)
XLA Ops:
  7.2 0.0 all-gather.4.cloned.1.call-start
  7.2 1.8 convert_convert_fusion
  9.0 0.0 all-gather.4.cloned.1.call-update
  9.1 0.0 reduce-scatter.4.cloned.1.call-start
  9.1 0.7 fusion.18
  9.8 0.7 fusion.17
  10.4 19.1 %all-gather.4.cloned.1.call-done = bf16[4096,128]{1,0:T(8,128)(2,1)} async-done(((bf16[1024,128]{1,0:T(8,128)(2,1)}), bf16[4096,128]{1,0:T(8,128)(2,1)}) %all-gather.4.cloned.1.call-update) | async-done | bytes 1048592 | tf_op jit(solution)/shard_map/all_gather | solution.py:28
  29.6 7.8 %gather_fusion = bf16[128,256,128]{2,1,0:T(8,128)(2,1)} fusion(bf16[16,256,128]{2,1,0:T(8,128)(2,1)} %bitcast.39, s32[1024]{0:T(1024)S(1)} %pad_clamp_fusion), kind=kCustom, calls=%fused_computation | custom fusion | bytes 16777728 | tf_op jit(solution)/shard_map/gather | solution.py:30
  37.3 17.2 %fusion.6 = f32[128,256,128]{1,2,0:T(8,128)} fusion(bf16[128,256,128]{2,1,0:T(8,128)(2,1)} %gather_fusion, bf16[1,1,128,256,256]{4,3,2,1,0:T(8,128)(2,1)} %param.5), kind=kOutput, calls=%fused_computation.12 | convolution fusion | flops 2147483648 | bytes 41943040 | tf_op jit(solution)/shard_map/kab,kbp->kap/dot_general | solution.py:31
  54.5 17.4 %copy.11 = f32[128,256,128]{2,1,0:T(8,128)} copy(f32[128,256,128]{1,2,0:T(8,128)} %fusion.6) | data formatting | bytes 33554432 | tf_op jit(solution)/shard_map/kab,kbp->kap/dot_general | solution.py:31
  71.9 0.2 broadcast.45.clone
  72.1 0.0 copy-start
  72.1 0.0 copy-start.3
  72.1 24.3 %scatter_fusion = f32[16,256,128]{2,1,0:T(8,128)S(1)} fusion(f32[16,256,128]{2,1,0:T(8,128)S(1)} %broadcast.45.clone, s32[128]{0:T(128)S(1)} %fusion.17, f32[128,256,128]{2,1,0:T(8,128)} %copy.11), kind=kCustom, calls=%fused_computation.3 | custom fusion | flops 4194304 | bytes 50332160 | tf_op jit(solution)/shard_map/scatter-add | solution.py:35
  96.5 1.2 convert_element_type.41
  97.7 0.0 reduce-scatter.4.cloned.1.call-update
  97.7 0.0 all-gather.6.cloned.1.call-start
  97.7 27.4 %reduce-scatter.4.cloned.1.call-done = bf16[1024,128]{1,0:T(8,128)(2,1)} async-done(((bf16[4096,128]{1,0:T(8,128)(2,1)}), bf16[1024,128]{1,0:T(8,128)(2,1)}) %reduce-scatter.4.cloned.1.call-update) | async-done | bytes 262160 | tf_op jit(solution)/shard_map/reduce_scatter | solution.py:37
  125.1 0.0 copy-done
  125.1 0.0 copy-done.3
  125.1 1.9 fusion.15
  127.0 0.0 all-gather.6.cloned.1.call-update
  127.0 0.0 reduce-scatter.6.cloned.1.call-start
  127.0 15.5 %all-gather.6.cloned.1.call-done = bf16[4096,128]{1,0:T(8,128)(2,1)} async-done(((bf16[1024,128]{1,0:T(8,128)(2,1)}), bf16[4096,128]{1,0:T(8,128)(2,1)}) %all-gather.6.cloned.1.call-update) | async-done | bytes 1048592 | tf_op jit(solution)/shard_map/all_gather | solution.py:28
  142.5 7.8 %gather_fusion.1 = bf16[128,256,128]{2,1,0:T(8,128)(2,1)} fusion(bf16[16,256,128]{2,1,0:T(8,128)(2,1)} %bitcast.41, s32[1024]{0:T(1024)S(1)} %pad_clamp_fusion), kind=kCustom, calls=%fused_computation.1 | custom fusion | bytes 16777728 | tf_op jit(solution)/shard_map/gather | solution.py:30
  150.3 17.2 %fusion.9 = f32[128,256,128]{1,2,0:T(8,128)} fusion(bf16[128,256,128]{2,1,0:T(8,128)(2,1)} %gather_fusion.1, bf16[1,1,128,256,256]{4,3,2,1,0:T(8,128)(2,1)} %param.5), kind=kOutput, calls=%fused_computation.13 | convolution fusion | flops 2147483648 | bytes 41943040 | tf_op jit(solution)/shard_map/kab,kbp->kap/dot_general | solution.py:31
  167.4 17.4 %copy.13 = f32[128,256,128]{2,1,0:T(8,128)} copy(f32[128,256,128]{1,2,0:T(8,128)} %fusion.9) | data formatting | bytes 33554432 | tf_op jit(solution)/shard_map/kab,kbp->kap/dot_general | solution.py:31
  184.8 0.2 broadcast.45.clone.1
  185.1 0.0 copy-start.1
  185.1 24.3 %scatter_fusion.1 = f32[16,256,128]{2,1,0:T(8,128)S(1)} fusion(f32[16,256,128]{2,1,0:T(8,128)S(1)} %broadcast.45.clone.1, s32[128]{0:T(128)S(1)} %fusion.17, f32[128,256,128]{2,1,0:T(8,128)} %copy.13), kind=kCustom, calls=%fused_computation.4 | custom fusion | flops 4194304 | bytes 50332160 | tf_op jit(solution)/shard_map/scatter-add | solution.py:35
  209.4 1.2 convert_element_type.45
  210.6 0.0 reduce-scatter.6.cloned.1.call-update
  210.6 0.0 all-gather.8.cloned.1.call-start
  210.6 27.4 %reduce-scatter.6.cloned.1.call-done = bf16[1024,128]{1,0:T(8,128)(2,1)} async-done(((bf16[4096,128]{1,0:T(8,128)(2,1)}), bf16[1024,128]{1,0:T(8,128)(2,1)}) %reduce-scatter.6.cloned.1.call-update) | async-done | bytes 262160 | tf_op jit(solution)/shard_map/reduce_scatter | solution.py:37
  238.0 0.0 copy-done.1
  238.0 1.9 fusion.16
  239.9 0.0 all-gather.8.cloned.1.call-update
  240.0 0.2 reduce-scatter.8.cloned.1.call-start
  240.2 15.1 %all-gather.8.cloned.1.call-done = bf16[4096,128]{1,0:T(8,128)(2,1)} async-done(((bf16[1024,128]{1,0:T(8,128)(2,1)}), bf16[4096,128]{1,0:T(8,128)(2,1)}) %all-gather.8.cloned.1.call-update) | async-done | bytes 1048592 | tf_op jit(solution)/shard_map/all_gather | solution.py:28
  255.3 7.8 %gather_fusion.2 = bf16[128,256,128]{2,1,0:T(8,128)(2,1)} fusion(bf16[16,256,128]{2,1,0:T(8,128)(2,1)} %bitcast.40, s32[1024]{0:T(1024)S(1)} %pad_clamp_fusion), kind=kCustom, calls=%fused_computation.2 | custom fusion | bytes 16777728 | tf_op jit(solution)/shard_map/gather | solution.py:30
  263.1 17.2 %fusion.12 = f32[128,256,128]{1,2,0:T(8,128)} fusion(bf16[128,256,128]{2,1,0:T(8,128)(2,1)} %gather_fusion.2, bf16[1,1,128,256,256]{4,3,2,1,0:T(8,128)(2,1)} %param.5), kind=kOutput, calls=%fused_computation.14 | convolution fusion | flops 2147483648 | bytes 41943040 | tf_op jit(solution)/shard_map/kab,kbp->kap/dot_general | solution.py:31
  280.3 17.4 %copy.15 = f32[128,256,128]{2,1,0:T(8,128)} copy(f32[128,256,128]{1,2,0:T(8,128)} %fusion.12) | data formatting | bytes 33554432 | tf_op jit(solution)/shard_map/kab,kbp->kap/dot_general | solution.py:31
  297.7 0.2 broadcast.45
  297.9 0.0 copy-start.2
  297.9 24.3 %scatter_fusion.2 = f32[16,256,128]{2,1,0:T(8,128)S(1)} fusion(f32[16,256,128]{2,1,0:T(8,128)S(1)} %broadcast.45, s32[128]{0:T(128)S(1)} %fusion.17, f32[128,256,128]{2,1,0:T(8,128)} %copy.15), kind=kCustom, calls=%fused_computation.5 | custom fusion | flops 4194304 | bytes 50332160 | tf_op jit(solution)/shard_map/scatter-add | solution.py:35
  322.2 1.2 convert_element_type.49
  323.4 0.0 reduce-scatter.8.cloned.1.call-update
  323.4 27.4 %reduce-scatter.8.cloned.1.call-done = bf16[1024,128]{1,0:T(8,128)(2,1)} async-done(((bf16[4096,128]{1,0:T(8,128)(2,1)}), bf16[1024,128]{1,0:T(8,128)(2,1)}) %reduce-scatter.8.cloned.1.call-update) | async-done | bytes 262160 | tf_op jit(solution)/shard_map/reduce_scatter | solution.py:37
  350.9 0.0 copy-done.2
  350.9 2.2 multiply_reduce_fusion.2
  353.0 6.2 %all-reduce = (f32[128]{0:T(128)S(1)}, f32[128]{0:T(128)S(1)}, f32[128]{0:T(128)S(1)}) all-reduce(f32[128]{0:T(128)S(1)} %get-tuple-element.4, f32[128]{0:T(128)S(1)} %get-tuple-element.3, f32[128]{0:T(128)S(1)} %get-tuple-element.2), channel_id=1, replica_groups=mesh['gx'=4,'gy'=4,'gz'=2] {'gy'}, use_global_device_ids=true, to_apply=%region_13.0 | all-reduce | flops 384 | bytes 3072 | tf_op jit(solution)/shard_map/psum | solution.py:9
  359.2 9.2 %all-reduce.1 = (f32[1,128]{1,0:T(1,128)S(1)}, f32[1,128]{1,0:T(1,128)S(1)}, f32[1,128]{1,0:T(1,128)S(1)}) all-reduce(f32[1,128]{1,0:T(1,128)S(1)} %bitcast.45, f32[1,128]{1,0:T(1,128)S(1)} %bitcast.46, f32[1,128]{1,0:T(1,128)S(1)} %bitcast.47), channel_id=1, replica_groups=mesh['gx'=4,'gy'=4,'gz'=2] {'gx'}, use_global_device_ids=true, to_apply=%region_14.0 | all-reduce | flops 384 | bytes 3072 | tf_op jit(solution)/shard_map/psum | solution.py:10
  368.4 0.6 pad_maximum_fusion
  (1 shorter events, 0.0 us)
Async XLA Ops:
  7.2 22.4 %all-gather.4.cloned.1.call-start = ((), (), s32[]{:S(2)}) async-start(), calls=%async_computation.3 | async-start | bytes 1310720 | tf_op jit(solution)/shard_map/all_gather | solution.py:28
  9.1 116.0 %reduce-scatter.4.cloned.1.call-start = ((), (), s32[]{:S(2)}) async-start(), calls=%async_computation.4 | async-start | bytes 1310720 | tf_op jit(solution)/shard_map/reduce_scatter | solution.py:37
  72.1 53.0 %copy-start = (s32[1024,128]{1,0:T(8,128)S(1)}, s32[1024,128]{1,0:T(8,128)}, u32[]{:S(2)}) copy-start(s32[1024,128]{1,0:T(8,128)} %param.8) | copy-start | bytes 1572868
  72.1 53.0 %copy-start.3 = (f32[1024]{0:T(1024)S(1)}, f32[1024]{0:T(1024)}, u32[]{:S(2)}) copy-start(f32[1024]{0:T(1024)} %param.9) | copy-start | bytes 12292
  97.7 44.8 %all-gather.6.cloned.1.call-start = ((), (), s32[]{:S(2)}) async-start(), calls=%async_computation.5 | async-start | bytes 1310720 | tf_op jit(solution)/shard_map/all_gather | solution.py:28
  127.0 111.0 %reduce-scatter.6.cloned.1.call-start = ((), (), s32[]{:S(2)}) async-start(), calls=%async_computation.6 | async-start | bytes 1310720 | tf_op jit(solution)/shard_map/reduce_scatter | solution.py:37
  185.1 53.0 %copy-start.1 = (bf16[1024,128]{1,0:T(8,128)(2,1)S(1)}, bf16[1024,128]{1,0:T(8,128)(2,1)}, u32[]{:S(2)}) copy-start(bf16[1024,128]{1,0:T(8,128)(2,1)} %reduce-scatter.4.cloned.1.call-done) | copy-start | bytes 786436
  210.6 44.7 %all-gather.8.cloned.1.call-start = ((), (), s32[]{:S(2)}) async-start(), calls=%async_computation.7 | async-start | bytes 1310720 | tf_op jit(solution)/shard_map/all_gather | solution.py:28
  240.0 110.9 %reduce-scatter.8.cloned.1.call-start = ((), (), s32[]{:S(2)}) async-start(), calls=%async_computation.8 | async-start | bytes 1310720 | tf_op jit(solution)/shard_map/reduce_scatter | solution.py:37
  297.9 53.0 %copy-start.2 = (bf16[1024,128]{1,0:T(8,128)(2,1)S(1)}, bf16[1024,128]{1,0:T(8,128)(2,1)}, u32[]{:S(2)}) copy-start(bf16[1024,128]{1,0:T(8,128)(2,1)} %reduce-scatter.6.cloned.1.call-done) | copy-start | bytes 786436
Sparse Core Ops, SparseCore 0:
  10.1 19.4 all-gather.3
  97.8 27.2 reduce-scatter.3
  127.2 15.2 all-gather.5
  210.7 27.2 reduce-scatter.5
  240.1 15.1 all-gather.7
  323.6 27.2 reduce-scatter.7
